TPU v7x, 32 devices: a whole 2x2x4 slice. The times are simulated.
32 devices in a mesh: tm: 4 (over y, core), space: 8 (over z, x).
Axes of the slice: x: 2, y: 2, z: 4, core: 2. Of those that a mesh axis runs over, the one named last changes fastest.
Arguments:
- state: float32 [4, 4, 16, 128, 128], P('tm', None, 'space'), may hold values from -6 to 6
- source: float32 [4, 4, 16, 128, 128], P('tm', None, 'space'), may hold values from -6 to 6
- start_field: float32 [16, 128, 128], P('space'), may hold values from -6 to 6
- diffusion: float32 [16, 128, 128], P('space'), may hold values from 0.1 to 1
- reaction: float32 [16, 128, 128], P('space'), may hold values from 0.3 to 3
- section_matrix: float32 [4, 4], replicated, may hold values from -0.5 to 3.5, as said below
- end_weights: float32 [4], replicated, may hold values from 0.2 to 0.6
Outputs:
- smoothed: float32 [4, 4, 16, 128, 128], P('tm', None, 'space')
Inputs may be any that keep to these rules, and one draw needn't show every extreme that they name: `section_matrix`: diagonal entries lie between 2 and 3.5, the others between -0.5 and 0.5.
All inputs are finite; a program needn't handle non-finite values.
Results may differ from a plain program's by a relative error of at most 0.0001.
Values sent between devices are 32-bit elements; how exact they have to be, the bound alone decides.
No kernel may reach another device: no remote copies, remote signals or barrier semaphores. Data moves between devices by JAX's collectives and lax.ppermute only.
A program may use at most 64 MiB of HBM per device.

v0:
```python
import jax
import jax.numpy as jnp
from jax import lax
from jax.sharding import PartitionSpec as P


def shifted(value, axis, steps):
    count = lax.axis_size(axis)
    first, last = (max(0, -steps), min(count, count - steps))
    return lax.ppermute(value, axis, [(source, source + steps) for source in range(first, last)])


def extended(x, sides, width):
    for axis, dim in sides:
        size, length = (lax.axis_size(axis), x.shape[dim])
        up = [(i, (i + 1) % size) for i in range(size - 1)]
        down = [(j, i) for i, j in up]
        last = lax.slice_in_dim(x, length - width, length, axis=dim)
        first = lax.slice_in_dim(x, 0, width, axis=dim)
        before = lax.ppermute(last, axis, up)
        after = lax.ppermute(first, axis, down)
        x = jnp.concatenate([before, x, after], axis=dim)
    return x


def swapped(x, axis, stride):
    return lax.ppermute(x, axis, [(i, i ^ 1 << stride) for i in range(lax.axis_size(axis))])


def laplace(padded):
    center = padded[:, :, 1:-1]
    side = padded[:, :, 2:] + padded[:, :, :-2]
    inner = jnp.pad(center, ((0, 0), (0, 0), (0, 0), (1, 1), (1, 1)))
    side = side + inner[:, :, :, 2:, 1:-1] + inner[:, :, :, :-2, 1:-1]
    side = side + inner[:, :, :, 1:-1, 2:] + inner[:, :, :, 1:-1, :-2]
    return 6.0 * center - side


def section_mix(section_matrix, field):
    return jnp.einsum("sr,nrxyz->nsxyz", section_matrix, field, precision=lax.Precision.HIGHEST)


def end_values(end_weights, field):
    return jnp.einsum("r,nrxyz->nxyz", end_weights, field, precision=lax.Precision.HIGHEST)


def fine_apply(field, section_matrix, end_weights, start_field, diffusion, reaction):
    ends = end_values(end_weights, field)
    arrived = shifted(ends, "tm", 1)
    before = jnp.where(lax.axis_index("tm") == 0, start_field[None], arrived)
    padded = extended(field, (("space", 2),), 1)
    return (
        section_mix(section_matrix, field)
        + diffusion * laplace(padded)
        + reaction * jnp.tanh(field)
        - before[:, None]
    )


def coarse_apply(own, whole, rows, end_weights, diffusion, reaction):
    ends = end_values(end_weights, whole)
    before = shifted(ends, "tm", 2)
    padded = extended(own, (("space", 2),), 1)
    return (
        section_mix(rows, whole)
        + 2.0 * (diffusion * laplace(padded) + reaction * own)
        - before[:, None]
    )


def trade_halves(piece):
    return swapped(piece, "tm", 0)


def joined(own, other, parity):
    lower = jnp.concatenate([own, other], 1)
    upper = jnp.concatenate([other, own], 1)
    return jnp.where(parity == 0, lower, upper)


def local(state, source, start_field, diffusion, reaction, section_matrix, end_weights):
    diag = jnp.diagonal(section_matrix)
    dfine = diag[None, :, None, None, None] + 6.0 * diffusion + reaction
    field = state
    for weight in (0.6, 1.0):
        field = (
            field
            + weight
            * (
                source
                - fine_apply(field, section_matrix, end_weights, start_field, diffusion, reaction)
            )
            / dfine
        )
    res = source - fine_apply(field, section_matrix, end_weights, start_field, diffusion, reaction)
    parity = lax.axis_index("tm") % 2
    half_count = res.shape[1] // 2
    own_start = parity * half_count
    other_start = (1 - parity) * half_count
    mine = lax.dynamic_slice_in_dim(res, own_start, half_count, 1)
    theirs = lax.dynamic_slice_in_dim(res, other_start, half_count, 1)
    coarse_res = mine + trade_halves(theirs)
    rows = lax.dynamic_slice_in_dim(section_matrix, own_start, half_count, 0)
    own_diag = lax.dynamic_slice_in_dim(diag, own_start, half_count, 0)
    dcoarse = own_diag[None, :, None, None, None] + 2.0 * (6.0 * diffusion + reaction)
    own = 0.7 * coarse_res / dcoarse
    for weight in (1.0, 0.7):
        whole = joined(own, trade_halves(own), parity)
        own = (
            own
            + weight
            * (coarse_res - coarse_apply(own, whole, rows, end_weights, diffusion, reaction))
            / dcoarse
        )
    correction = joined(own, trade_halves(own), parity)
    field = field + correction
    for weight in (1.0, 0.6):
        field = (
            field
            + weight
            * (
                source
                - fine_apply(field, section_matrix, end_weights, start_field, diffusion, reaction)
            )
            / dfine
        )
    return field


def solution(mesh):
    in_specs = (
        P("tm", None, "space", None, None),
        P("tm", None, "space", None, None),
        P("space", None, None),
        P("space", None, None),
        P("space", None, None),
        P(),
        P(),
    )
    out_specs = P("tm", None, "space", None, None)
    return jax.shard_map(local, mesh=mesh, in_specs=in_specs, out_specs=out_specs, check_vma=False)
```

profile of v0, /device:TPU:0, one launch (start us, length us, event | category | flops | bytes accessed | tf_op | source)
XLA Modules:
  0.0 155.2 jit_solution(2602041097080106875)
XLA Ops:
  6.6 5.0 %collective-permute-start.1 = (f32[1,4,1,128,128]{4,1,3,2,0:T(4,128)S(1)}, f32[1,4,1,128,128]{4,1,3,2,0:T(4,128)S(1)}, u32[]{:S(2)}, u32[]{:S(2)}) collective-permute-start(f32[1,4,1,128,128]{4,1,3,2,0:T(4,128)S(1)} %get-tuple-element.16), channel_id=1, source_target_pairs={{0,1},{1,2},{2,3},{3,4},{4,5},{5,6},{6,7},{8,9},{9,10},{10,11},{11... | collective-permute-start | bytes 786440 | tf_op jit(solution)/shard_map/ppermute | solution.py:20
  12.4 2.9 %collective-permute-done = f32[1,4,1,128,128]{4,1,3,2,0:T(4,128)S(1)} collective-permute-done((f32[1,4,1,128,128]{4,1,3,2,0:T(4,128)S(1)}, f32[1,4,1,128,128]{4,1,3,2,0:T(4,128)S(1)}, u32[]{:S(2)}, u32[]{:S(2)}) %collective-permute-start) | collective-permute-done | bytes 262176 | tf_op jit(solution)/shard_map/ppermute | solution.py:21
  15.4 7.3 %collective-permute-done.1 = f32[1,4,1,128,128]{4,1,3,2,0:T(4,128)S(1)} collective-permute-done((f32[1,4,1,128,128]{4,1,3,2,0:T(4,128)S(1)}, f32[1,4,1,128,128]{4,1,3,2,0:T(4,128)S(1)}, u32[]{:S(2)}, u32[]{:S(2)}) %collective-permute-start.1) | collective-permute-done | bytes 262176 | tf_op jit(solution)/shard_map/ppermute | solution.py:20
  22.7 3.3 %fusion.31 = f32[1,4,2,128,128]{4,1,3,2,0:T(4,128)S(1)} fusion(f32[1,4,2,128,128]{4,1,3,2,0:T(4,128)S(1)} %copy.32, f32[1,4,1,128,128]{4,1,3,2,0:T(4,128)S(1)} %collective-permute-done.1, f32[1,4,1,128,128]{4,1,3,2,0:T(4,128)S(1)} %collective-permute-done, f32[4,2,128,128]{3,2,1,0:T(8,128)S(1)} %bitcast.236, f32[1,4,2,128,128]{4,3,2,1,0:T(8,128)S(1)} %copy-done.6, ...), kind=kOutput, calls=%fused_computation.67 | convolution fusion | flops 8912896 | bytes 3145808 | tf_op jit(solution)/shard_map/sr,nrxyz->nsxyz/dot_general | solution.py:40
  30.6 4.8 %collective-permute-start.4 = (f32[1,4,1,128,128]{4,1,3,2,0:T(4,128)S(1)}, f32[1,4,1,128,128]{4,1,3,2,0:T(4,128)S(1)}, u32[]{:S(2)}, u32[]{:S(2)}) collective-permute-start(f32[1,4,1,128,128]{4,1,3,2,0:T(4,128)S(1)} %get-tuple-element.14), channel_id=1, source_target_pairs={{0,1},{1,2},{2,3},{3,4},{4,5},{5,6},{6,7},{8,9},{9,10},{10,11},{11... | collective-permute-start | bytes 786440 | tf_op jit(solution)/shard_map/ppermute | solution.py:20
  35.4 4.5 %collective-permute-done.3 = f32[1,4,1,128,128]{4,1,3,2,0:T(4,128)S(1)} collective-permute-done((f32[1,4,1,128,128]{4,1,3,2,0:T(4,128)S(1)}, f32[1,4,1,128,128]{4,1,3,2,0:T(4,128)S(1)}, u32[]{:S(2)}, u32[]{:S(2)}) %collective-permute-start.3) | collective-permute-done | bytes 262176 | tf_op jit(solution)/shard_map/ppermute | solution.py:21
  39.9 5.8 %collective-permute-done.4 = f32[1,4,1,128,128]{4,1,3,2,0:T(4,128)S(1)} collective-permute-done((f32[1,4,1,128,128]{4,1,3,2,0:T(4,128)S(1)}, f32[1,4,1,128,128]{4,1,3,2,0:T(4,128)S(1)}, u32[]{:S(2)}, u32[]{:S(2)}) %collective-permute-start.4) | collective-permute-done | bytes 262176 | tf_op jit(solution)/shard_map/ppermute | solution.py:20
  45.7 2.7 %fusion.41 = f32[1,4,2,128,128]{4,1,3,2,0:T(4,128)S(1)} fusion(f32[1,4,2,128,128]{4,1,3,2,0:T(4,128)S(1)} %fusion.31, f32[1,4,1,128,128]{4,1,3,2,0:T(4,128)S(1)} %collective-permute-done.4, f32[1,4,1,128,128]{4,1,3,2,0:T(4,128)S(1)} %collective-permute-done.3, f32[1,4,2,128,128]{4,3,2,1,0:T(8,128)S(1)} %copy-done.6, f32[2,128,128]{2,1,0:T(8,128)S(1)} %fusion.103, ...), kind=kOutput, calls=%fused_computation.77 | convolution fusion | flops 8781824 | bytes 3148288 | tf_op jit(solution)/shard_map/sr,nrxyz->nsxyz/dot_general | solution.py:40
  52.7 5.0 %collective-permute-start.7 = (f32[1,4,1,128,128]{4,1,3,2,0:T(4,128)S(1)}, f32[1,4,1,128,128]{4,1,3,2,0:T(4,128)S(1)}, u32[]{:S(2)}, u32[]{:S(2)}) collective-permute-start(f32[1,4,1,128,128]{4,1,3,2,0:T(4,128)S(1)} %get-tuple-element.12), channel_id=1, source_target_pairs={{0,1},{1,2},{2,3},{3,4},{4,5},{5,6},{6,7},{8,9},{9,10},{10,11},{11... | collective-permute-start | bytes 786440 | tf_op jit(solution)/shard_map/ppermute | solution.py:20
  57.8 4.5 %collective-permute-done.6 = f32[1,4,1,128,128]{4,1,3,2,0:T(4,128)S(1)} collective-permute-done((f32[1,4,1,128,128]{4,1,3,2,0:T(4,128)S(1)}, f32[1,4,1,128,128]{4,1,3,2,0:T(4,128)S(1)}, u32[]{:S(2)}, u32[]{:S(2)}) %collective-permute-start.6) | collective-permute-done | bytes 262176 | tf_op jit(solution)/shard_map/ppermute | solution.py:21
  62.3 5.8 %collective-permute-done.7 = f32[1,4,1,128,128]{4,1,3,2,0:T(4,128)S(1)} collective-permute-done((f32[1,4,1,128,128]{4,1,3,2,0:T(4,128)S(1)}, f32[1,4,1,128,128]{4,1,3,2,0:T(4,128)S(1)}, u32[]{:S(2)}, u32[]{:S(2)}) %collective-permute-start.7) | collective-permute-done | bytes 262176 | tf_op jit(solution)/shard_map/ppermute | solution.py:20
  73.7 5.2 %collective-permute-start.12 = (f32[1,2,1,128,128]{4,1,3,2,0:T(2,128)S(1)}, f32[1,2,1,128,128]{4,1,3,2,0:T(2,128)S(1)}, u32[]{:S(2)}, u32[]{:S(2)}) collective-permute-start(f32[1,2,1,128,128]{4,1,3,2,0:T(2,128)S(1)} %get-tuple-element.20), channel_id=1, source_target_pairs={{0,1},{1,2},{2,3},{3,4},{4,5},{5,6},{6,7},{8,9},{9,10},{10,11},{11... | collective-permute-start | bytes 393224 | tf_op jit(solution)/shard_map/ppermute | solution.py:20
  88.9 5.2 %collective-permute-start.16 = (f32[1,2,1,128,128]{4,1,3,2,0:T(2,128)S(1)}, f32[1,2,1,128,128]{4,1,3,2,0:T(2,128)S(1)}, u32[]{:S(2)}, u32[]{:S(2)}) collective-permute-start(f32[1,2,1,128,128]{4,1,3,2,0:T(2,128)S(1)} %get-tuple-element.18), channel_id=1, source_target_pairs={{0,1},{1,2},{2,3},{3,4},{4,5},{5,6},{6,7},{8,9},{9,10},{10,11},{11... | collective-permute-start | bytes 393224 | tf_op jit(solution)/shard_map/ppermute | solution.py:20
  95.4 4.4 %collective-permute-start.17 = (f32[1,2,128,128]{3,2,1,0:T(8,128)S(1)}, f32[1,2,128,128]{3,2,1,0:T(8,128)S(1)}, u32[]{:S(2)}, u32[]{:S(2)}) collective-permute-start(f32[1,2,128,128]{3,2,1,0:T(8,128)S(1)} %bitcast.253), channel_id=1, source_target_pairs={{0,16},{8,24},{1,17},{9,25},{2,18},{10,26},{3,19},{11,27},{4,20},{... | collective-permute-start | bytes 393224 | tf_op jit(solution)/shard_map/ppermute | solution.py:10
  99.9 3.1 %collective-permute-done.17 = f32[1,2,128,128]{3,2,1,0:T(8,128)S(1)} collective-permute-done((f32[1,2,128,128]{3,2,1,0:T(8,128)S(1)}, f32[1,2,128,128]{3,2,1,0:T(8,128)S(1)}, u32[]{:S(2)}, u32[]{:S(2)}) %collective-permute-start.17) | collective-permute-done | bytes 131104 | tf_op jit(solution)/shard_map/ppermute | solution.py:10
  102.9 2.6 %fusion.20 = f32[1,2,2,128,128]{4,1,3,2,0:T(2,128)S(1)} fusion(f32[1,2,2,128,128]{4,1,3,2,0:T(2,128)S(1)} %fusion.14, f32[1,2,2,128,128]{4,1,3,2,0:T(2,128)S(1)} %get-tuple-element.6, f32[1,2,1,128,128]{4,1,3,2,0:T(2,128)S(1)} %collective-permute-done.16, f32[1,2,1,128,128]{4,1,3,2,0:T(2,128)S(1)} %collective-permute-done.15, ...), kind=kOutput, calls=%fused_computation.48 | convolution fusion | flops 4849664 | bytes 2098693 | tf_op jit(solution)/shard_map/sr,nrxyz->nsxyz/dot_general | solution.py:40
  112.0 5.2 %collective-permute-start.20 = (f32[1,4,1,128,128]{4,1,3,2,0:T(4,128)S(1)}, f32[1,4,1,128,128]{4,1,3,2,0:T(4,128)S(1)}, u32[]{:S(2)}, u32[]{:S(2)}) collective-permute-start(f32[1,4,1,128,128]{4,1,3,2,0:T(4,128)S(1)} %get-tuple-element.10), channel_id=1, source_target_pairs={{0,1},{1,2},{2,3},{3,4},{4,5},{5,6},{6,7},{8,9},{9,10},{10,11},{11... | collective-permute-start | bytes 786440 | tf_op jit(solution)/shard_map/ppermute | solution.py:20
  117.2 3.4 %collective-permute-done.19 = f32[1,4,1,128,128]{4,1,3,2,0:T(4,128)S(1)} collective-permute-done((f32[1,4,1,128,128]{4,1,3,2,0:T(4,128)S(1)}, f32[1,4,1,128,128]{4,1,3,2,0:T(4,128)S(1)}, u32[]{:S(2)}, u32[]{:S(2)}) %collective-permute-start.19) | collective-permute-done | bytes 262176 | tf_op jit(solution)/shard_map/ppermute | solution.py:21
  120.6 7.7 %collective-permute-done.20 = f32[1,4,1,128,128]{4,1,3,2,0:T(4,128)S(1)} collective-permute-done((f32[1,4,1,128,128]{4,1,3,2,0:T(4,128)S(1)}, f32[1,4,1,128,128]{4,1,3,2,0:T(4,128)S(1)}, u32[]{:S(2)}, u32[]{:S(2)}) %collective-permute-start.20) | collective-permute-done | bytes 262176 | tf_op jit(solution)/shard_map/ppermute | solution.py:20
  128.3 2.7 %fusion.59 = f32[1,4,2,128,128]{4,1,3,2,0:T(4,128)S(1)} fusion(f32[1,4,2,128,128]{4,1,3,2,0:T(4,128)S(1)} %fusion.76, f32[1,4,1,128,128]{4,1,3,2,0:T(4,128)S(1)} %collective-permute-done.20, f32[1,4,1,128,128]{4,1,3,2,0:T(4,128)S(1)} %collective-permute-done.19, f32[1,4,2,128,128]{4,3,2,1,0:T(8,128)S(1)} %copy-done.6, f32[2,128,128]{2,1,0:T(8,128)S(1)} %fusion.105, ...), kind=kOutput, calls=%fused_computation.95 | convolution fusion | flops 8781824 | bytes 3148288 | tf_op jit(solution)/shard_map/sr,nrxyz->nsxyz/dot_general | solution.py:40
  135.6 4.8 %collective-permute-start.23 = (f32[1,4,1,128,128]{4,1,3,2,0:T(4,128)S(1)}, f32[1,4,1,128,128]{4,1,3,2,0:T(4,128)S(1)}, u32[]{:S(2)}, u32[]{:S(2)}) collective-permute-start(f32[1,4,1,128,128]{4,1,3,2,0:T(4,128)S(1)} %get-tuple-element.8), channel_id=1, source_target_pairs={{0,1},{1,2},{2,3},{3,4},{4,5},{5,6},{6,7},{8,9},{9,10},{10,11},{11... | collective-permute-start | bytes 786440 | tf_op jit(solution)/shard_map/ppermute | solution.py:20
  140.5 4.9 %collective-permute-done.22 = f32[1,4,1,128,128]{4,1,3,2,0:T(4,128)S(1)} collective-permute-done((f32[1,4,1,128,128]{4,1,3,2,0:T(4,128)S(1)}, f32[1,4,1,128,128]{4,1,3,2,0:T(4,128)S(1)}, u32[]{:S(2)}, u32[]{:S(2)}) %collective-permute-start.22) | collective-permute-done | bytes 262176 | tf_op jit(solution)/shard_map/ppermute | solution.py:21
  145.4 6.3 %collective-permute-done.23 = f32[1,4,1,128,128]{4,1,3,2,0:T(4,128)S(1)} collective-permute-done((f32[1,4,1,128,128]{4,1,3,2,0:T(4,128)S(1)}, f32[1,4,1,128,128]{4,1,3,2,0:T(4,128)S(1)}, u32[]{:S(2)}, u32[]{:S(2)}) %collective-permute-start.23) | collective-permute-done | bytes 262176 | tf_op jit(solution)/shard_map/ppermute | solution.py:20
  151.7 2.6 %fusion.70 = f32[1,4,2,128,128]{4,1,3,2,0:T(4,128)S(1)} fusion(f32[1,4,2,128,128]{4,1,3,2,0:T(4,128)S(1)} %fusion.59, f32[1,4,1,128,128]{4,1,3,2,0:T(4,128)S(1)} %collective-permute-done.23, f32[1,4,1,128,128]{4,1,3,2,0:T(4,128)S(1)} %collective-permute-done.22, f32[1,4,2,128,128]{4,3,2,1,0:T(8,128)S(1)} %copy-done.6, f32[2,128,128]{2,1,0:T(8,128)S(1)} %fusion.106, ...), kind=kOutput, calls=%fused_computation.106 | convolution fusion | flops 8912896 | bytes 3148288 | tf_op jit(solution)/shard_map/sr,nrxyz->nsxyz/dot_general | solution.py:40
  (75 shorter events, 44.9 us)
Async XLA Ops:
  2.4 10.0 %collective-permute-start.2 = (f32[1,2,128,128]{3,2,1,0:T(8,128)S(1)}, f32[1,2,128,128]{3,2,1,0:T(8,128)S(1)}, u32[]{:S(2)}, u32[]{:S(2)}) collective-permute-start(f32[1,2,128,128]{3,2,1,0:T(8,128)S(1)} %bitcast.242), channel_id=1, source_target_pairs={{0,8},{8,16},{16,24},{1,9},{9,17},{17,25},{2,10},{10,18},{18,26},{... | collective-permute-start | bytes 393224 | tf_op jit(solution)/shard_map/ppermute | solution.py:10
  5.2 10.2 %collective-permute-start = (f32[1,4,1,128,128]{4,1,3,2,0:T(4,128)S(1)}, f32[1,4,1,128,128]{4,1,3,2,0:T(4,128)S(1)}, u32[]{:S(2)}, u32[]{:S(2)}) collective-permute-start(f32[1,4,1,128,128]{4,1,3,2,0:T(4,128)S(1)} %get-tuple-element.15), channel_id=1, source_target_pairs={{1,0},{2,1},{3,2},{4,3},{5,4},{6,5},{7,6},{9,8},{10,9},{11,10},{12... | collective-permute-start | bytes 786440 | tf_op jit(solution)/shard_map/ppermute | solution.py:21
  6.6 16.0 %collective-permute-start.1 = (f32[1,4,1,128,128]{4,1,3,2,0:T(4,128)S(1)}, f32[1,4,1,128,128]{4,1,3,2,0:T(4,128)S(1)}, u32[]{:S(2)}, u32[]{:S(2)}) collective-permute-start(f32[1,4,1,128,128]{4,1,3,2,0:T(4,128)S(1)} %get-tuple-element.16), channel_id=1, source_target_pairs={{0,1},{1,2},{2,3},{3,4},{4,5},{5,6},{6,7},{8,9},{9,10},{10,11},{11... | collective-permute-start | bytes 786440 | tf_op jit(solution)/shard_map/ppermute | solution.py:20
  27.0 8.4 %collective-permute-start.5 = (f32[1,2,128,128]{3,2,1,0:T(8,128)S(1)}, f32[1,2,128,128]{3,2,1,0:T(8,128)S(1)}, u32[]{:S(2)}, u32[]{:S(2)}) collective-permute-start(f32[1,2,128,128]{3,2,1,0:T(8,128)S(1)} %bitcast.243), channel_id=1, source_target_pairs={{0,8},{8,16},{16,24},{1,9},{9,17},{17,25},{2,10},{10,18},{18,26},{... | collective-permute-start | bytes 393224 | tf_op jit(solution)/shard_map/ppermute | solution.py:10
  29.3 10.7 %collective-permute-start.3 = (f32[1,4,1,128,128]{4,1,3,2,0:T(4,128)S(1)}, f32[1,4,1,128,128]{4,1,3,2,0:T(4,128)S(1)}, u32[]{:S(2)}, u32[]{:S(2)}) collective-permute-start(f32[1,4,1,128,128]{4,1,3,2,0:T(4,128)S(1)} %get-tuple-element.13), channel_id=1, source_target_pairs={{1,0},{2,1},{3,2},{4,3},{5,4},{6,5},{7,6},{9,8},{10,9},{11,10},{12... | collective-permute-start | bytes 786440 | tf_op jit(solution)/shard_map/ppermute | solution.py:21
  30.6 15.2 %collective-permute-start.4 = (f32[1,4,1,128,128]{4,1,3,2,0:T(4,128)S(1)}, f32[1,4,1,128,128]{4,1,3,2,0:T(4,128)S(1)}, u32[]{:S(2)}, u32[]{:S(2)}) collective-permute-start(f32[1,4,1,128,128]{4,1,3,2,0:T(4,128)S(1)} %get-tuple-element.14), channel_id=1, source_target_pairs={{0,1},{1,2},{2,3},{3,4},{4,5},{5,6},{6,7},{8,9},{9,10},{10,11},{11... | collective-permute-start | bytes 786440 | tf_op jit(solution)/shard_map/ppermute | solution.py:20
  49.4 8.3 %collective-permute-start.8 = (f32[1,2,128,128]{3,2,1,0:T(8,128)S(1)}, f32[1,2,128,128]{3,2,1,0:T(8,128)S(1)}, u32[]{:S(2)}, u32[]{:S(2)}) collective-permute-start(f32[1,2,128,128]{3,2,1,0:T(8,128)S(1)} %bitcast.241), channel_id=1, source_target_pairs={{0,8},{8,16},{16,24},{1,9},{9,17},{17,25},{2,10},{10,18},{18,26},{... | collective-permute-start | bytes 393224 | tf_op jit(solution)/shard_map/ppermute | solution.py:10
  51.4 10.9 %collective-permute-start.6 = (f32[1,4,1,128,128]{4,1,3,2,0:T(4,128)S(1)}, f32[1,4,1,128,128]{4,1,3,2,0:T(4,128)S(1)}, u32[]{:S(2)}, u32[]{:S(2)}) collective-permute-start(f32[1,4,1,128,128]{4,1,3,2,0:T(4,128)S(1)} %get-tuple-element.11), channel_id=1, source_target_pairs={{1,0},{2,1},{3,2},{4,3},{5,4},{6,5},{7,6},{9,8},{10,9},{11,10},{12... | collective-permute-start | bytes 786440 | tf_op jit(solution)/shard_map/ppermute | solution.py:21
  52.7 15.3 %collective-permute-start.7 = (f32[1,4,1,128,128]{4,1,3,2,0:T(4,128)S(1)}, f32[1,4,1,128,128]{4,1,3,2,0:T(4,128)S(1)}, u32[]{:S(2)}, u32[]{:S(2)}) collective-permute-start(f32[1,4,1,128,128]{4,1,3,2,0:T(4,128)S(1)} %get-tuple-element.12), channel_id=1, source_target_pairs={{0,1},{1,2},{2,3},{3,4},{4,5},{5,6},{6,7},{8,9},{9,10},{10,11},{11... | collective-permute-start | bytes 786440 | tf_op jit(solution)/shard_map/ppermute | solution.py:20
  70.2 1.6 %collective-permute-start.9 = (f32[1,2,2,128,128]{4,1,3,2,0:T(2,128)S(1)}, f32[1,2,2,128,128]{4,1,3,2,0:T(2,128)S(1)}, u32[]{:S(2)}, u32[]{:S(2)}) collective-permute-start(f32[1,2,2,128,128]{4,1,3,2,0:T(2,128)S(1)} %constant_dynamic-slice_fusion.1), channel_id=1, source_target_pairs={{0,8},{8,0},{16,24},{24,16},{1,9},{9,1},{17,25},{25,17},{2,10},{10... | collective-permute-start | bytes 786440 | tf_op jit(solution)/shard_map/ppermute | solution.py:27
  72.2 6.7 %collective-permute-start.10 = (f32[1,2,2,128,128]{4,1,3,2,0:T(2,128)S(1)}, f32[1,2,2,128,128]{4,1,3,2,0:T(2,128)S(1)}, u32[]{:S(2)}, u32[]{:S(2)}) collective-permute-start(f32[1,2,2,128,128]{4,1,3,2,0:T(2,128)S(1)} %get-tuple-element.5), channel_id=1, source_target_pairs={{0,8},{8,0},{16,24},{24,16},{1,9},{9,1},{17,25},{25,17},{2,10},{10... | collective-permute-start | bytes 786440 | tf_op jit(solution)/shard_map/ppermute | solution.py:27
  72.4 9.2 %collective-permute-start.11 = (f32[1,2,1,128,128]{4,1,3,2,0:T(2,128)S(1)}, f32[1,2,1,128,128]{4,1,3,2,0:T(2,128)S(1)}, u32[]{:S(2)}, u32[]{:S(2)}) collective-permute-start(f32[1,2,1,128,128]{4,1,3,2,0:T(2,128)S(1)} %get-tuple-element.19), channel_id=1, source_target_pairs={{1,0},{2,1},{3,2},{4,3},{5,4},{6,5},{7,6},{9,8},{10,9},{11,10},{12... | collective-permute-start | bytes 393224 | tf_op jit(solution)/shard_map/ppermute | solution.py:21
  73.7 10.1 %collective-permute-start.12 = (f32[1,2,1,128,128]{4,1,3,2,0:T(2,128)S(1)}, f32[1,2,1,128,128]{4,1,3,2,0:T(2,128)S(1)}, u32[]{:S(2)}, u32[]{:S(2)}) collective-permute-start(f32[1,2,1,128,128]{4,1,3,2,0:T(2,128)S(1)} %get-tuple-element.20), channel_id=1, source_target_pairs={{0,1},{1,2},{2,3},{3,4},{4,5},{5,6},{6,7},{8,9},{9,10},{10,11},{11... | collective-permute-start | bytes 393224 | tf_op jit(solution)/shard_map/ppermute | solution.py:20
  80.3 4.6 %collective-permute-start.13 = (f32[1,2,128,128]{3,2,1,0:T(8,128)S(1)}, f32[1,2,128,128]{3,2,1,0:T(8,128)S(1)}, u32[]{:S(2)}, u32[]{:S(2)}) collective-permute-start(f32[1,2,128,128]{3,2,1,0:T(8,128)S(1)} %bitcast.252), channel_id=1, source_target_pairs={{0,16},{8,24},{1,17},{9,25},{2,18},{10,26},{3,19},{11,27},{4,20},{... | collective-permute-start | bytes 393224 | tf_op jit(solution)/shard_map/ppermute | solution.py:10
  87.5 6.6 %collective-permute-start.14 = (f32[1,2,2,128,128]{4,1,3,2,0:T(2,128)S(1)}, f32[1,2,2,128,128]{4,1,3,2,0:T(2,128)S(1)}, u32[]{:S(2)}, u32[]{:S(2)}) collective-permute-start(f32[1,2,2,128,128]{4,1,3,2,0:T(2,128)S(1)} %fusion.14), channel_id=1, source_target_pairs={{0,8},{8,0},{16,24},{24,16},{1,9},{9,1},{17,25},{25,17},{2,10},{10... | collective-permute-start | bytes 786440 | tf_op jit(solution)/shard_map/ppermute | solution.py:27
  87.6 12.3 %collective-permute-start.15 = (f32[1,2,1,128,128]{4,1,3,2,0:T(2,128)S(1)}, f32[1,2,1,128,128]{4,1,3,2,0:T(2,128)S(1)}, u32[]{:S(2)}, u32[]{:S(2)}) collective-permute-start(f32[1,2,1,128,128]{4,1,3,2,0:T(2,128)S(1)} %get-tuple-element.17), channel_id=1, source_target_pairs={{1,0},{2,1},{3,2},{4,3},{5,4},{6,5},{7,6},{9,8},{10,9},{11,10},{12... | collective-permute-start | bytes 393224 | tf_op jit(solution)/shard_map/ppermute | solution.py:21
  88.9 11.0 %collective-permute-start.16 = (f32[1,2,1,128,128]{4,1,3,2,0:T(2,128)S(1)}, f32[1,2,1,128,128]{4,1,3,2,0:T(2,128)S(1)}, u32[]{:S(2)}, u32[]{:S(2)}) collective-permute-start(f32[1,2,1,128,128]{4,1,3,2,0:T(2,128)S(1)} %get-tuple-element.18), channel_id=1, source_target_pairs={{0,1},{1,2},{2,3},{3,4},{4,5},{5,6},{6,7},{8,9},{9,10},{10,11},{11... | collective-permute-start | bytes 393224 | tf_op jit(solution)/shard_map/ppermute | solution.py:20
  95.4 7.5 %collective-permute-start.17 = (f32[1,2,128,128]{3,2,1,0:T(8,128)S(1)}, f32[1,2,128,128]{3,2,1,0:T(8,128)S(1)}, u32[]{:S(2)}, u32[]{:S(2)}) collective-permute-start(f32[1,2,128,128]{3,2,1,0:T(8,128)S(1)} %bitcast.253), channel_id=1, source_target_pairs={{0,16},{8,24},{1,17},{9,25},{2,18},{10,26},{3,19},{11,27},{4,20},{... | collective-permute-start | bytes 393224 | tf_op jit(solution)/shard_map/ppermute | solution.py:10
  108.6 8.6 %collective-permute-start.21 = (f32[1,2,128,128]{3,2,1,0:T(8,128)S(1)}, f32[1,2,128,128]{3,2,1,0:T(8,128)S(1)}, u32[]{:S(2)}, u32[]{:S(2)}) collective-permute-start(f32[1,2,128,128]{3,2,1,0:T(8,128)S(1)} %bitcast.244), channel_id=1, source_target_pairs={{0,8},{8,16},{16,24},{1,9},{9,17},{17,25},{2,10},{10,18},{18,26},{... | collective-permute-start | bytes 393224 | tf_op jit(solution)/shard_map/ppermute | solution.py:10
  110.7 9.9 %collective-permute-start.19 = (f32[1,4,1,128,128]{4,1,3,2,0:T(4,128)S(1)}, f32[1,4,1,128,128]{4,1,3,2,0:T(4,128)S(1)}, u32[]{:S(2)}, u32[]{:S(2)}) collective-permute-start(f32[1,4,1,128,128]{4,1,3,2,0:T(4,128)S(1)} %get-tuple-element.9), channel_id=1, source_target_pairs={{1,0},{2,1},{3,2},{4,3},{5,4},{6,5},{7,6},{9,8},{10,9},{11,10},{12... | collective-permute-start | bytes 786440 | tf_op jit(solution)/shard_map/ppermute | solution.py:21
  112.0 16.3 %collective-permute-start.20 = (f32[1,4,1,128,128]{4,1,3,2,0:T(4,128)S(1)}, f32[1,4,1,128,128]{4,1,3,2,0:T(4,128)S(1)}, u32[]{:S(2)}, u32[]{:S(2)}) collective-permute-start(f32[1,4,1,128,128]{4,1,3,2,0:T(4,128)S(1)} %get-tuple-element.10), channel_id=1, source_target_pairs={{0,1},{1,2},{2,3},{3,4},{4,5},{5,6},{6,7},{8,9},{9,10},{10,11},{11... | collective-permute-start | bytes 786440 | tf_op jit(solution)/shard_map/ppermute | solution.py:20
  132.1 8.4 %collective-permute-start.24 = (f32[1,2,128,128]{3,2,1,0:T(8,128)S(1)}, f32[1,2,128,128]{3,2,1,0:T(8,128)S(1)}, u32[]{:S(2)}, u32[]{:S(2)}) collective-permute-start(f32[1,2,128,128]{3,2,1,0:T(8,128)S(1)} %bitcast.245), channel_id=1, source_target_pairs={{0,8},{8,16},{16,24},{1,9},{9,17},{17,25},{2,10},{10,18},{18,26},{... | collective-permute-start | bytes 393224 | tf_op jit(solution)/shard_map/ppermute | solution.py:10
  134.3 11.1 %collective-permute-start.22 = (f32[1,4,1,128,128]{4,1,3,2,0:T(4,128)S(1)}, f32[1,4,1,128,128]{4,1,3,2,0:T(4,128)S(1)}, u32[]{:S(2)}, u32[]{:S(2)}) collective-permute-start(f32[1,4,1,128,128]{4,1,3,2,0:T(4,128)S(1)} %get-tuple-element.7), channel_id=1, source_target_pairs={{1,0},{2,1},{3,2},{4,3},{5,4},{6,5},{7,6},{9,8},{10,9},{11,10},{12... | collective-permute-start | bytes 786440 | tf_op jit(solution)/shard_map/ppermute | solution.py:21
  135.6 16.1 %collective-permute-start.23 = (f32[1,4,1,128,128]{4,1,3,2,0:T(4,128)S(1)}, f32[1,4,1,128,128]{4,1,3,2,0:T(4,128)S(1)}, u32[]{:S(2)}, u32[]{:S(2)}) collective-permute-start(f32[1,4,1,128,128]{4,1,3,2,0:T(4,128)S(1)} %get-tuple-element.8), channel_id=1, source_target_pairs={{0,1},{1,2},{2,3},{3,4},{4,5},{5,6},{6,7},{8,9},{9,10},{10,11},{11... | collective-permute-start | bytes 786440 | tf_op jit(solution)/shard_map/ppermute | solution.py:20
  (8 other events, 51.1 us)
where the time goes:
time: 156 us; the launch traced here: 155 us
  waiting for transfers between devices  62.4 us (40%)
  starting transfers between devices  61.4 us (39%)
  matrix products  27.7 us (18%)
  local copies, waits for them, and re-layouts  2.28 us (1%)
    ppermute x7, starting transfers between devices, extended(): before = lax.ppermute(last, axis, up)  35.2 us
    ppermute x7, waiting for transfers between devices, extended(): before = lax.ppermute(last, axis, up)  35.1 us
    ppermute x7, waiting for transfers between devices, extended(): after = lax.ppermute(first, axis, down)  20.2 us
    dot_general x7, matrix products, section_mix(): jnp.einsum('sr,nrxyz->nsxyz', section_matrix, field, precision=lax.Precis...  18.5 us
    ppermute x7, starting transfers between devices, shifted(): lax.ppermute(value, axis, [(source, source + steps) for source in range(f...  16.5 us
    ppermute x7, starting transfers between devices, extended(): after = lax.ppermute(first, axis, down)  9.18 us
    dot_general x7, matrix products, end_values(): jnp.einsum('r,nrxyz->nxyz', end_weights, field, precision=lax.Precision.H...  9.15 us
    ppermute x7, waiting for transfers between devices, shifted(): lax.ppermute(value, axis, [(source, source + steps) for source in range(f...  4.18 us
  transfers between devices with their start and end apart: 25, of which 15 were waited for; matrix products, arithmetic and copies ran while one was open for 3% of the time, Pallas kernels for 0%

commit v1 on v0

v1 whole, which is shorter than its diff:
```python
import functools

import jax
import jax.numpy as jnp
from jax import lax
from jax.experimental import pallas as pl
from jax.experimental.pallas import tpu as pltpu
from jax.sharding import PartitionSpec as P

HALO = 8
SUB = 8

VMEM = pl.BlockSpec(memory_space=pltpu.VMEM)
SMEM = pl.BlockSpec(memory_space=pltpu.SMEM)
ANY = pl.BlockSpec(memory_space=pl.ANY)
F32 = jnp.float32


def permutations(slabs, blocks):
    ys, zs = slabs // 2, blocks // 2

    def at(y, c, z, x):
        return (2 * y + c) * blocks + 2 * z + x

    everyone = [(y, c, z, x) for y in range(ys) for c in range(2) for z in range(zs) for x in range(2)]

    def depth(y, c, z, x):
        if c == 1:
            return at(y, 0, z + 1, x) if z + 1 < zs else at(y, 1, z, 1 - x)
        return at(y, 1, z - 1, x) if z > 0 else at(y, 0, z, 1 - x)

    maps = {
        "first": lambda y, c, z, x: at(y, x, z, c),
        "second": lambda y, c, z, x: at(y, x, z, 1 - c),
        "back": lambda y, c, z, x: at(y, 1 - x, z, c),
        "depth": depth,
        "core": lambda y, c, z, x: at(y, 1 - c, z, x),
        "time": lambda y, c, z, x: at((y + 1) % ys, c, z, x),
    }
    return {name: [(at(*d), move(*d)) for d in everyone] for name, move in maps.items()}


def call(body, ins, outs, scratch=(), name=None):
    specs = [spec for spec, _ in ins]
    return pl.pallas_call(
        body,
        in_specs=specs,
        out_specs=[spec for spec, _ in outs],
        out_shape=[jax.ShapeDtypeStruct(shape, F32) for _, shape in outs],
        scratch_shapes=list(scratch),
        compiler_params=pltpu.CompilerParams(vmem_limit_bytes=8 << 20),
        name=name,
    )(*[value for _, value in ins])


def run_copies(copies, sems):
    started = [pltpu.make_async_copy(src, dst, sems.at[i]) for i, (src, dst) in enumerate(copies)]
    for copy in started:
        copy.start()
    for copy in started:
        copy.wait()


def pack_kernel(flags, field, *refs):
    coefs, (first, second, sems) = refs[:-3], refs[-3:]
    core, x = flags[0], flags[1]
    sections, rows = field.shape[1], first.shape[-2]
    step = field.shape[3] - rows
    copies = []
    for target, half in ((first, core), (second, 1 - core)):
        start = pl.multiple_of(half * step, SUB)
        for slot, plane in ((0, x), (1, 1 - x)):
            copies.append((field.at[0, :, plane, pl.ds(start, rows)], target.at[slot, pl.ds(0, sections)]))
    start = pl.multiple_of((1 - core) * step, SUB)
    for index, coef in enumerate(coefs):
        for slot, plane in ((0, x), (1, 1 - x)):
            copies.append((coef.at[plane, pl.ds(start, rows)], second.at[slot, sections + index]))
    run_copies(copies, sems)


def chunks(rows):
    return [(k, pl.ds(k * SUB, SUB)) for k in range(rows // SUB)]


def order_kernel(flags, weights, first, second, outer, inner, ends):
    x = flags[1]
    sections = outer.shape[1]
    for slot, target in ((0, outer), (1, inner)):
        for _, rows in chunks(outer.shape[2]):
            for s in range(sections):
                target[x, s, rows] = first[slot, s, rows]
                target[1 - x, s, rows] = second[slot, s, rows]
        for _, rows in chunks(outer.shape[2]):
            ends[slot, rows] = sum(weights[s] * target[1, s, rows] for s in range(sections))


def scale_kernel(flags, matrix, first, second, *outs):
    x = flags[1]
    sections = first.shape[1]
    for slot in range(2):
        source, coefs, fine, coarse = outs[4 * slot : 4 * slot + 4]
        for _, rows in chunks(first.shape[2]):
            for s in range(sections):
                source[x, s, rows] = first[slot, s, rows]
                source[1 - x, s, rows] = second[slot, s, rows]
            for index in range(3):
                coefs[index, rows] = second[slot, sections + index, rows]
            base = 6.0 * second[slot, sections, rows] + second[slot, sections + 1, rows]
            for s in range(sections):
                fine[s, rows] = 1.0 / (matrix[s, s] + base)
                coarse[s, rows] = 1.0 / (matrix[s, s] + 2.0 * base)


def edges():
    lane = lax.broadcasted_iota(jnp.int32, (SUB, 128), 1)
    row = lax.broadcasted_iota(jnp.int32, (SUB, 128), 0)
    return lane == 0, lane == 127, row == 0, row == SUB - 1


def around(read, total, k, center, masks):
    left, right, top, bottom = masks
    lanes = center.shape[1]
    near = jnp.where(left, 0.0, pltpu.roll(center, 1, 1)) + jnp.where(right, 0.0, pltpu.roll(center, lanes - 1, 1))
    if k == 0:
        above = jnp.where(top, 0.0, pltpu.roll(center, 1, 0))
    else:
        above = read(pl.ds(k * SUB - 1, SUB))
    if k == total - 1:
        below = jnp.where(bottom, 0.0, pltpu.roll(center, SUB - 1, 0))
    else:
        below = read(pl.ds(k * SUB + 1, SUB))
    return near + (above + below)


def off_mix(matrix, s, values):
    return sum(matrix[s, r] * values[r] for r in range(len(values)) if r != s)


def weighted(weights, values):
    return sum(weights[r] * value for r, value in enumerate(values))


def fine_kernel(flags, matrix, weights, field, other, halo, arrived, source, coefs, scale, *refs, slot, weight, last):
    total = field.shape[2] // SUB
    sections = field.shape[1]
    masks = edges()
    x, begins = flags[1], flags[2] == 1
    inside = flags[3].astype(F32)
    for k, rows in chunks(field.shape[2]):
        diffusion, reaction = coefs[0, rows], coefs[1, rows]
        values = [[field[n, s, rows] for s in range(sections)] for n in range(2)]
        befores = [jnp.where(begins, coefs[2, rows], arrived[slot, rows]), weighted(weights, values[0])]
        updated = []
        for n in range(2):
            for s in range(sections):
                value = values[n][s]
                beside = halo[n, s, rows]
                if slot == 0:
                    beside = beside * inside
                near = around(lambda at, n=n, s=s: field[n, s, at], total, k, value, masks)
                near = near + (other[n, s, rows] + beside)
                acc = (source[n, s, rows] + befores[n]) + diffusion * near
                acc = acc - off_mix(matrix, s, values[n]) - reaction * (jnp.tanh(value) - value)
                new = scale[s, rows] * acc
                if weight != 1.0:
                    new = (1.0 - weight) * value + weight * new
                updated.append(new)
        if not last:
            out = refs[-2]
            for n in range(2):
                for s in range(sections):
                    out[n, s, rows] = updated[n * sections + s]
            ends = weighted(weights, updated[sections:])
            if slot == 0:
                refs[-1][0, rows] = ends
                refs[-1][1, rows] = refs[0][rows]
            else:
                refs[-1][rows] = ends
        else:
            out = refs[-1]

            def put(rows=rows, k=k, updated=updated, out=out):
                place = pl.ds(pl.multiple_of((k - x) * SUB, SUB), SUB)
                for n in range(2):
                    for s in range(sections):
                        out[n, s, place] = updated[n * sections + s]

            if k == 0:
                pl.when(x == 0)(put)
            elif k == total - 1:
                pl.when(x == 1)(put)
            else:
                put()


def residual_kernel(flags, matrix, weights, field, other, halo, arrived, source, coefs, scale, *refs, slot):
    total = field.shape[2] // SUB
    sections = field.shape[1]
    masks = edges()
    begins = flags[2] == 1
    inside = flags[3].astype(F32)
    kept, out = refs[-3], refs[-2]
    for k, rows in chunks(field.shape[2]):
        diffusion, reaction = coefs[0, rows], coefs[1, rows]
        firsts = [field[0, s, rows] for s in range(sections)]
        seconds = [field[1, s, rows] for s in range(sections)]
        both = [a + b for a, b in zip(firsts, seconds)]
        before = jnp.where(begins, coefs[2, rows], arrived[slot, rows]) + weighted(weights, firsts)
        made = []
        for s in range(sections):
            beside = halo[0, s, rows] + halo[1, s, rows]
            if slot == 0:
                beside = beside * inside
            near = around(lambda at, s=s: field[0, s, at] + field[1, s, at], total, k, both[s], masks)
            near = near + (other[0, s, rows] + other[1, s, rows] + beside)
            acc = (source[0, s, rows] + source[1, s, rows]) + before + diffusion * (near - 6.0 * both[s])
            acc = acc - (off_mix(matrix, s, both) + matrix[s, s] * both[s])
            acc = acc - reaction * (jnp.tanh(firsts[s]) + jnp.tanh(seconds[s]))
            kept[s, rows] = acc
            new = 0.7 * (acc * scale[s, rows])
            out[s, rows] = new
            made.append(new)
        ends = weighted(weights, made)
        if slot == 0:
            refs[-1][0, rows] = ends
            refs[-1][1, rows] = refs[0][rows]
        else:
            refs[-1][rows] = ends


def coarse_kernel(flags, matrix, weights, field, other, halo, arrived, source, coefs, scale, *refs, slot, weight, last):
    total = field.shape[1] // SUB
    sections = field.shape[0]
    masks = edges()
    continues = flags[2] == 0
    inside = flags[3].astype(F32)
    for k, rows in chunks(field.shape[1]):
        double = 2.0 * coefs[0, rows]
        values = [field[s, rows] for s in range(sections)]
        before = jnp.where(continues, arrived[slot, rows], 0.0)
        made = []
        for s in range(sections):
            beside = halo[s, rows]
            if slot == 0:
                beside = beside * inside
            near = around(lambda at, s=s: field[s, at], total, k, values[s], masks)
            near = near + (other[s, rows] + beside)
            acc = (source[s, rows] + before) + double * near - off_mix(matrix, s, values)
            new = scale[s, rows] * acc
            if weight != 1.0:
                new = (1.0 - weight) * values[s] + weight * new
            made.append(new)
        out = refs[-2]
        if last:
            fine = refs[0]
            for n in range(2):
                for s in range(sections):
                    out[n, s, rows] = fine[n, s, rows] + made[s]
            made = [fine[1, s, rows] + made[s] for s in range(sections)]
        else:
            for s in range(sections):
                out[s, rows] = made[s]
        ends = weighted(weights, made)
        if slot == 0:
            refs[-1][0, rows] = ends
            refs[-1][1, rows] = refs[1 if last else 0][rows]
        else:
            refs[-1][rows] = ends


def split_kernel(flags, field, first, second):
    x = flags[1]
    for _, rows in chunks(field.shape[2]):
        for s in range(field.shape[1]):
            first[s, rows] = field[x, s, rows]
            second[s, rows] = field[1 - x, s, rows]


def place_kernel(flags, first_outer, second_outer, first_inner, second_inner, out, sems):
    core, x = flags[0], flags[1]
    half = first_outer.shape[1]
    copies = []
    for plane, parts in ((x, (first_outer, second_outer)), (1 - x, (first_inner, second_inner))):
        for part, which in zip(parts, (core, 1 - core)):
            start = pl.multiple_of(which * half, SUB)
            copies.append((part, out.at[0, :, plane, pl.ds(start, half)]))
    run_copies(copies, sems)


def local(state, source, start_field, diffusion, reaction, matrix, weights, moves):
    sections, ny, nz = state.shape[1], state.shape[3], state.shape[4]
    half = ny // 2
    rows = half + HALO
    tm, space = lax.axis_index("tm"), lax.axis_index("space")
    core, x = tm % 2, space % 2
    outermost = jnp.where(core == 0, space // 2 == 0, space // 2 == lax.axis_size("space") // 2 - 1)
    flags = jnp.stack([core, x, (tm // 2 == 0).astype(jnp.int32), 1 - outermost.astype(jnp.int32)]).astype(jnp.int32)

    def move(value, name):
        return lax.ppermute(value, ("tm", "space"), moves[name])

    small = [(SMEM, flags)]
    both = [(SMEM, flags), (SMEM, matrix), (SMEM, weights)]
    plane, pair = (sections, rows, nz), (2, sections, rows, nz)

    first, second = call(
        pack_kernel, small + [(ANY, state)], [(VMEM, (2, sections, rows, nz))] * 2, [pltpu.SemaphoreType.DMA((4,))], name="pack_state"
    )
    first, second = move(first, "first"), move(second, "second")
    more, rest = call(
        pack_kernel,
        small + [(ANY, source), (ANY, diffusion), (ANY, reaction), (ANY, start_field)],
        [(VMEM, (2, sections, rows, nz)), (VMEM, (2, sections + 3, rows, nz))],
        [pltpu.SemaphoreType.DMA((10,))],
        name="pack_source",
    )
    more, rest = move(more, "first"), move(rest, "second")
    outer, inner, ends = call(
        order_kernel,
        small + [(SMEM, weights), (VMEM, first), (VMEM, second)],
        [(VMEM, pair), (VMEM, pair), (VMEM, (2, rows, nz))],
        name="order",
    )
    source_o, coefs_o, fine_o, coarse_o, source_i, coefs_i, fine_i, coarse_i = call(
        scale_kernel,
        small + [(SMEM, matrix), (VMEM, more), (VMEM, rest)],
        [(VMEM, pair), (VMEM, (3, rows, nz)), (VMEM, plane), (VMEM, plane)] * 2,
        name="scale",
    )

    def step(body, outer, inner, ends, source_o, source_i, scale_o, scale_i, extra, outs, name):
        depth, beside, arrived = move(outer, "depth"), move(inner, "core"), move(ends, "time")
        made_i = call(
            functools.partial(body, slot=1),
            both + [(VMEM, v) for v in (inner, outer, beside, arrived, source_i, coefs_i, scale_i)] + [(VMEM, v) for v in extra[1]],
            [(VMEM, shape) for shape in outs] + [(VMEM, (rows, nz))],
            name=name + "_inner",
        )
        made_o = call(
            functools.partial(body, slot=0),
            both + [(VMEM, v) for v in (outer, inner, depth, arrived, source_o, coefs_o, scale_o)] + [(VMEM, v) for v in extra[0]] + [(VMEM, made_i[-1])],
            [(VMEM, shape) for shape in outs] + [(VMEM, (2, rows, nz))],
            name=name + "_outer",
        )
        return made_o, made_i

    none = ((), ())

    def fine(outer, inner, ends, weight):
        made_o, made_i = step(
            functools.partial(fine_kernel, weight=weight, last=False),
            outer, inner, ends, source_o, source_i, fine_o, fine_i, none, [pair], "fine",
        )
        return made_o[0], made_i[0], made_o[1]

    for weight in (0.6, 1.0):
        outer, inner, ends = fine(outer, inner, ends, weight)
    made_o, made_i = step(
        residual_kernel, outer, inner, ends, source_o, source_i, coarse_o, coarse_i, none, [plane, plane], "residual"
    )
    kept_o, kept_i = made_o[0], made_i[0]
    made_o, made_i = step(
        functools.partial(coarse_kernel, weight=1.0, last=False),
        made_o[1], made_i[1], made_o[2], kept_o, kept_i, coarse_o, coarse_i, none, [plane], "coarse",
    )
    made_o, made_i = step(
        functools.partial(coarse_kernel, weight=0.7, last=True),
        made_o[0], made_i[0], made_o[1], kept_o, kept_i, coarse_o, coarse_i, ((outer,), (inner,)), [pair], "coarse_last",
    )
    outer, inner, ends = fine(made_o[0], made_i[0], made_o[1], 1.0)

    depth, beside, arrived = move(outer, "depth"), move(inner, "core"), move(ends, "time")
    body = functools.partial(fine_kernel, weight=0.6, last=True)
    parts = []
    for slot, args in ((1, (inner, outer, beside, arrived, source_i, coefs_i, fine_i)), (0, (outer, inner, depth, arrived, source_o, coefs_o, fine_o))):
        (made,) = call(
            functools.partial(body, slot=slot), both + [(VMEM, v) for v in args], [(VMEM, (2, sections, half, nz))], name=f"last_{slot}"
        )
        first, second = call(split_kernel, small + [(VMEM, made)], [(VMEM, (sections, half, nz))] * 2, name=f"split_{slot}")
        parts.append((move(first, "first"), move(second, "back")))
    (out,) = call(
        place_kernel, small + [(VMEM, v) for v in parts[1] + parts[0]], [(ANY, state.shape)], [pltpu.SemaphoreType.DMA((4,))], name="place"
    )
    return out


def solution(mesh):
    moves = permutations(mesh.shape["tm"], mesh.shape["space"])
    in_specs = (
        P("tm", None, "space", None, None),
        P("tm", None, "space", None, None),
        P("space", None, None),
        P("space", None, None),
        P("space", None, None),
        P(),
        P(),
    )
    out_specs = P("tm", None, "space", None, None)
    body = functools.partial(local, moves=moves)
    return jax.shard_map(body, mesh=mesh, in_specs=in_specs, out_specs=out_specs, check_vma=False)
```

time: 156 us -> 85.6 us (0.55)
  waiting for transfers between devices: 62.4 us -> 29.7 us
  matrix products: 27.7 us -> 0 us
  starting transfers between devices: 61.4 us -> 34 us
  Pallas kernels: 0 us -> 17.6 us
    ppermute x25 -> x29, waiting for transfers between devices: 62.4 us -> 29.7 us  [move(): return lax.ppermute(value, ('tm', 'space'), moves[name])]
    dot_general x14 -> x0, matrix products: 27.7 us -> none  [the longest x7 18.5 us: section_mix(): jnp.einsum('sr,nrxyz->nsxyz', section_matrix, field, precision=lax.Precis...]
    ppermute x25 -> x29, starting transfers between devices: 61.4 us -> 34 us  [move(): return lax.ppermute(value, ('tm', 'space'), moves[name])]
    pallas_call x0 -> x21, Pallas kernels: none -> 17.6 us  [call(): pl.pallas_call(body, in_specs=specs, out_specs=[spec for spec, _ in outs]...]
    unnamed x15 -> x14, local copies, waits for them, and re-layouts: 0.38 us -> 3.77 us
  transfers between devices with their start and end apart: 25 -> 29, of which waited for: 15 -> 12; matrix products, arithmetic and copies ran while one was open for 3% -> 0% of each run, Pallas kernels for 0% -> 18%
where the time goes in v1:
time: 85.6 us; the launch traced here: 85.3 us
  starting transfers between devices  34 us (40%)
  waiting for transfers between devices  29.7 us (35%)
  Pallas kernels  17.6 us (21%)
  local copies, waits for them, and re-layouts  3.77 us (4%)
    ppermute x29, starting transfers between devices, move(): return lax.ppermute(value, ('tm', 'space'), moves[name])  34 us
    ppermute x29, waiting for transfers between devices, move(): return lax.ppermute(value, ('tm', 'space'), moves[name])  29.7 us
    pallas_call x21, Pallas kernels, call(): pl.pallas_call(body, in_specs=specs, out_specs=[spec for spec, _ in outs]...  17.6 us
    unnamed x14, local copies, waits for them, and re-layouts  3.77 us
  transfers between devices with their start and end apart: 29, of which 12 were waited for; matrix products, arithmetic and copies ran while one was open for 0% of the time, Pallas kernels for 18%

profile of v1, /device:TPU:0, one launch (start us, length us, event | category | flops | bytes accessed | tf_op | source)
XLA Modules:
  0.0 85.3 jit_solution(12729988528950117025)
XLA Ops:
  2.6 4.2 %collective-permute-start.1 = (f32[2,4,72,128]{3,2,1,0:T(8,128)S(1)}, f32[2,4,72,128]{3,2,1,0:T(8,128)S(1)}, u32[]{:S(2)}, u32[]{:S(2)}) collective-permute-start(f32[2,4,72,128]{3,2,1,0:T(8,128)S(1)} %get-tuple-element.51), channel_id=1, source_target_pairs={{0,1},{1,9},{2,3},{3,11},{4,5},{5,13},{6,7},{7,15},{8,0},{9,8},{10... | collective-permute-start | bytes 884744 | tf_op jit(solution)/shard_map/ppermute | solution.py:300
  11.4 2.2 %collective-permute-done.1.second = f32[2,4,72,128]{3,2,1,0:T(8,128)S(1)} collective-permute-done((f32[2,4,72,128]{3,2,1,0:T(8,128)S(1)}, f32[2,4,72,128]{3,2,1,0:T(8,128)S(1)}, u32[]{:S(2)}, u32[]{:S(2)}) %collective-permute-start.1) | collective-permute-done | bytes 294944 | tf_op jit(solution)/shard_map/ppermute | solution.py:300
  15.3 1.6 %collective-permute-start.2 = (f32[2,4,72,128]{3,2,1,0:T(8,128)S(1)}, f32[2,4,72,128]{3,2,1,0:T(8,128)S(1)}, u32[]{:S(2)}, u32[]{:S(2)}) collective-permute-start(f32[2,4,72,128]{3,2,1,0:T(8,128)S(1)} %get-tuple-element.52.other.field), channel_id=1, source_target_pairs={{0,1},{1,0},{2,8},{3,9},{4,10},{5,11},{6,12},{7,13},{8,2},{9,3},{1... | collective-permute-start | bytes 884744 | tf_op jit(solution)/shard_map/ppermute | solution.py:300
  16.9 1.5 %collective-permute-start.3 = (f32[2,72,128]{2,1,0:T(8,128)S(1)}, f32[2,72,128]{2,1,0:T(8,128)S(1)}, u32[]{:S(2)}, u32[]{:S(2)}) collective-permute-start(f32[2,72,128]{2,1,0:T(8,128)S(1)} %get-tuple-element.54), channel_id=1, source_target_pairs={{0,16},{1,17},{2,18},{3,19},{4,20},{5,21},{6,22},{7,23},{8,24},{9,... | collective-permute-start | bytes 221192 | tf_op jit(solution)/shard_map/ppermute | solution.py:300
  18.4 3.9 %collective-permute-done.5.second = f32[2,7,72,128]{3,2,1,0:T(8,128)S(1)} collective-permute-done((f32[2,7,72,128]{3,2,1,0:T(8,128)S(1)}, f32[2,7,72,128]{3,2,1,0:T(8,128)S(1)}, u32[]{:S(2)}, u32[]{:S(2)}) %collective-permute-start.5) | collective-permute-done | bytes 516128 | tf_op jit(solution)/shard_map/ppermute | solution.py:300
  23.9 2.0 %collective-permute-start.9 = (f32[2,4,72,128]{3,2,1,0:T(8,128)S(1)}, f32[2,4,72,128]{3,2,1,0:T(8,128)S(1)}, u32[]{:S(2)}, u32[]{:S(2)}) collective-permute-start(f32[2,4,72,128]{3,2,1,0:T(8,128)S(1)} %get-tuple-element.65.field.other), channel_id=1, source_target_pairs={{0,8},{1,9},{2,10},{3,11},{4,12},{5,13},{6,14},{7,15},{8,0},{9,1},... | collective-permute-start | bytes 884744 | tf_op jit(solution)/shard_map/ppermute | solution.py:300
  27.4 1.5 %collective-permute-start.7 = (f32[2,4,72,128]{3,2,1,0:T(8,128)S(1)}, f32[2,4,72,128]{3,2,1,0:T(8,128)S(1)}, u32[]{:S(2)}, u32[]{:S(2)}) collective-permute-start(f32[2,4,72,128]{3,2,1,0:T(8,128)S(1)} %get-tuple-element.64.other.field), channel_id=1, source_target_pairs={{0,1},{1,0},{2,8},{3,9},{4,10},{5,11},{6,12},{7,13},{8,2},{9,3},{1... | collective-permute-start | bytes 884744 | tf_op jit(solution)/shard_map/ppermute | solution.py:300
  28.9 1.5 %collective-permute-start.8 = (f32[2,72,128]{2,1,0:T(8,128)S(1)}, f32[2,72,128]{2,1,0:T(8,128)S(1)}, u32[]{:S(2)}, u32[]{:S(2)}) collective-permute-start(f32[2,72,128]{2,1,0:T(8,128)S(1)} %get-tuple-element.66), channel_id=1, source_target_pairs={{0,16},{1,17},{2,18},{3,19},{4,20},{5,21},{6,22},{7,23},{8,24},{9,... | collective-permute-start | bytes 221192 | tf_op jit(solution)/shard_map/ppermute | solution.py:300
  30.4 2.8 %collective-permute-done.8.arrived = f32[2,72,128]{2,1,0:T(8,128)S(1)} collective-permute-done((f32[2,72,128]{2,1,0:T(8,128)S(1)}, f32[2,72,128]{2,1,0:T(8,128)S(1)}, u32[]{:S(2)}, u32[]{:S(2)}) %collective-permute-start.8) | collective-permute-done | bytes 73760 | tf_op jit(solution)/shard_map/ppermute | solution.py:300
  35.1 1.5 %collective-permute-start.10 = (f32[2,4,72,128]{3,2,1,0:T(8,128)S(1)}, f32[2,4,72,128]{3,2,1,0:T(8,128)S(1)}, u32[]{:S(2)}, u32[]{:S(2)}) collective-permute-start(f32[2,4,72,128]{3,2,1,0:T(8,128)S(1)} %get-tuple-element.68.other.field.refs_0_), channel_id=1, source_target_pairs={{0,1},{1,0},{2,8},{3,9},{4,10},{5,11},{6,12},{7,13},{8,2},{9,3},{1... | collective-permute-start | bytes 884744 | tf_op jit(solution)/shard_map/ppermute | solution.py:300
  36.6 1.5 %collective-permute-start.11 = (f32[2,72,128]{2,1,0:T(8,128)S(1)}, f32[2,72,128]{2,1,0:T(8,128)S(1)}, u32[]{:S(2)}, u32[]{:S(2)}) collective-permute-start(f32[2,72,128]{2,1,0:T(8,128)S(1)} %get-tuple-element.70), channel_id=1, source_target_pairs={{0,16},{1,17},{2,18},{3,19},{4,20},{5,21},{6,22},{7,23},{8,24},{9,... | collective-permute-start | bytes 221192 | tf_op jit(solution)/shard_map/ppermute | solution.py:300
  38.1 2.8 %collective-permute-done.11.arrived = f32[2,72,128]{2,1,0:T(8,128)S(1)} collective-permute-done((f32[2,72,128]{2,1,0:T(8,128)S(1)}, f32[2,72,128]{2,1,0:T(8,128)S(1)}, u32[]{:S(2)}, u32[]{:S(2)}) %collective-permute-start.11) | collective-permute-done | bytes 73760 | tf_op jit(solution)/shard_map/ppermute | solution.py:300
  42.7 1.5 %collective-permute-start.13 = (f32[4,72,128]{2,1,0:T(8,128)S(1)}, f32[4,72,128]{2,1,0:T(8,128)S(1)}, u32[]{:S(2)}, u32[]{:S(2)}) collective-permute-start(f32[4,72,128]{2,1,0:T(8,128)S(1)} %get-tuple-element.74.other.field), channel_id=1, source_target_pairs={{0,1},{1,0},{2,8},{3,9},{4,10},{5,11},{6,12},{7,13},{8,2},{9,3},{1... | collective-permute-start | bytes 442376 | tf_op jit(solution)/shard_map/ppermute | solution.py:300
  44.2 1.5 %collective-permute-start.14 = (f32[2,72,128]{2,1,0:T(8,128)S(1)}, f32[2,72,128]{2,1,0:T(8,128)S(1)}, u32[]{:S(2)}, u32[]{:S(2)}) collective-permute-start(f32[2,72,128]{2,1,0:T(8,128)S(1)} %get-tuple-element.76), channel_id=1, source_target_pairs={{0,16},{1,17},{2,18},{3,19},{4,20},{5,21},{6,22},{7,23},{8,24},{9,... | collective-permute-start | bytes 221192 | tf_op jit(solution)/shard_map/ppermute | solution.py:300
  45.7 2.8 %collective-permute-done.14.arrived = f32[2,72,128]{2,1,0:T(8,128)S(1)} collective-permute-done((f32[2,72,128]{2,1,0:T(8,128)S(1)}, f32[2,72,128]{2,1,0:T(8,128)S(1)}, u32[]{:S(2)}, u32[]{:S(2)}) %collective-permute-start.14) | collective-permute-done | bytes 73760 | tf_op jit(solution)/shard_map/ppermute | solution.py:300
  50.9 1.5 %collective-permute-start.17 = (f32[2,72,128]{2,1,0:T(8,128)S(1)}, f32[2,72,128]{2,1,0:T(8,128)S(1)}, u32[]{:S(2)}, u32[]{:S(2)}) collective-permute-start(f32[2,72,128]{2,1,0:T(8,128)S(1)} %get-tuple-element.82), channel_id=1, source_target_pairs={{0,16},{1,17},{2,18},{3,19},{4,20},{5,21},{6,22},{7,23},{8,24},{9,... | collective-permute-start | bytes 221192 | tf_op jit(solution)/shard_map/ppermute | solution.py:300
  52.4 2.8 %collective-permute-done.17.arrived = f32[2,72,128]{2,1,0:T(8,128)S(1)} collective-permute-done((f32[2,72,128]{2,1,0:T(8,128)S(1)}, f32[2,72,128]{2,1,0:T(8,128)S(1)}, u32[]{:S(2)}, u32[]{:S(2)}) %collective-permute-start.17) | collective-permute-done | bytes 73760 | tf_op jit(solution)/shard_map/ppermute | solution.py:300
  56.9 1.4 %collective-permute-start.19 = (f32[2,4,72,128]{3,2,1,0:T(8,128)S(1)}, f32[2,4,72,128]{3,2,1,0:T(8,128)S(1)}, u32[]{:S(2)}, u32[]{:S(2)}) collective-permute-start(f32[2,4,72,128]{3,2,1,0:T(8,128)S(1)} %get-tuple-element.84.other.field), channel_id=1, source_target_pairs={{0,1},{1,0},{2,8},{3,9},{4,10},{5,11},{6,12},{7,13},{8,2},{9,3},{1... | collective-permute-start | bytes 884744 | tf_op jit(solution)/shard_map/ppermute | solution.py:300
  58.3 1.5 %collective-permute-start.20 = (f32[2,72,128]{2,1,0:T(8,128)S(1)}, f32[2,72,128]{2,1,0:T(8,128)S(1)}, u32[]{:S(2)}, u32[]{:S(2)}) collective-permute-start(f32[2,72,128]{2,1,0:T(8,128)S(1)} %get-tuple-element.86), channel_id=1, source_target_pairs={{0,16},{1,17},{2,18},{3,19},{4,20},{5,21},{6,22},{7,23},{8,24},{9,... | collective-permute-start | bytes 221192 | tf_op jit(solution)/shard_map/ppermute | solution.py:300
  59.8 2.8 %collective-permute-done.20.arrived = f32[2,72,128]{2,1,0:T(8,128)S(1)} collective-permute-done((f32[2,72,128]{2,1,0:T(8,128)S(1)}, f32[2,72,128]{2,1,0:T(8,128)S(1)}, u32[]{:S(2)}, u32[]{:S(2)}) %collective-permute-start.20) | collective-permute-done | bytes 73760 | tf_op jit(solution)/shard_map/ppermute | solution.py:300
  65.9 1.5 %collective-permute-start.23 = (f32[2,72,128]{2,1,0:T(8,128)S(1)}, f32[2,72,128]{2,1,0:T(8,128)S(1)}, u32[]{:S(2)}, u32[]{:S(2)}) collective-permute-start(f32[2,72,128]{2,1,0:T(8,128)S(1)} %get-tuple-element.90), channel_id=1, source_target_pairs={{0,16},{1,17},{2,18},{3,19},{4,20},{5,21},{6,22},{7,23},{8,24},{9,... | collective-permute-start | bytes 221192 | tf_op jit(solution)/shard_map/ppermute | solution.py:300
  67.5 2.8 %collective-permute-done.23.arrived = f32[2,72,128]{2,1,0:T(8,128)S(1)} collective-permute-done((f32[2,72,128]{2,1,0:T(8,128)S(1)}, f32[2,72,128]{2,1,0:T(8,128)S(1)}, u32[]{:S(2)}, u32[]{:S(2)}) %collective-permute-start.23) | collective-permute-done | bytes 73760 | tf_op jit(solution)/shard_map/ppermute | solution.py:300
  72.5 2.0 %collective-permute-start.28 = (f32[4,64,128]{2,1,0:T(8,128)S(1)}, f32[4,64,128]{2,1,0:T(8,128)S(1)}, u32[]{:S(2)}, u32[]{:S(2)}) collective-permute-start(f32[4,64,128]{2,1,0:T(8,128)S(1)} %get-tuple-element.94), channel_id=1, source_target_pairs={{0,8},{1,0},{2,10},{3,2},{4,12},{5,4},{6,14},{7,6},{8,9},{9,1},{10... | collective-permute-start | bytes 393224 | tf_op jit(solution)/shard_map/ppermute | solution.py:300
  78.7 5.2 %collective-permute-done.25.second_outer = f32[4,64,128]{2,1,0:T(8,128)S(1)} collective-permute-done((f32[4,64,128]{2,1,0:T(8,128)S(1)}, f32[4,64,128]{2,1,0:T(8,128)S(1)}, u32[]{:S(2)}, u32[]{:S(2)}) %collective-permute-start.25) | collective-permute-done | bytes 131104 | tf_op jit(solution)/shard_map/ppermute | solution.py:300
  (70 shorter events, 30.5 us)
Async XLA Ops:
  1.9 9.5 %collective-permute-start = (f32[2,4,72,128]{3,2,1,0:T(8,128)S(1)}, f32[2,4,72,128]{3,2,1,0:T(8,128)S(1)}, u32[]{:S(2)}, u32[]{:S(2)}) collective-permute-start(f32[2,4,72,128]{3,2,1,0:T(8,128)S(1)} %get-tuple-element.50), channel_id=1, source_target_pairs={{0,0},{1,8},{2,2},{3,10},{4,4},{5,12},{6,6},{7,14},{8,1},{9,9},{10... | collective-permute-start | bytes 884744 | tf_op jit(solution)/shard_map/ppermute | solution.py:300
  2.6 11.0 %collective-permute-start.1 = (f32[2,4,72,128]{3,2,1,0:T(8,128)S(1)}, f32[2,4,72,128]{3,2,1,0:T(8,128)S(1)}, u32[]{:S(2)}, u32[]{:S(2)}) collective-permute-start(f32[2,4,72,128]{3,2,1,0:T(8,128)S(1)} %get-tuple-element.51), channel_id=1, source_target_pairs={{0,1},{1,9},{2,3},{3,11},{4,5},{5,13},{6,7},{7,15},{8,0},{9,8},{10... | collective-permute-start | bytes 884744 | tf_op jit(solution)/shard_map/ppermute | solution.py:300
  10.7 11.6 %collective-permute-start.5 = (f32[2,7,72,128]{3,2,1,0:T(8,128)S(1)}, f32[2,7,72,128]{3,2,1,0:T(8,128)S(1)}, u32[]{:S(2)}, u32[]{:S(2)}) collective-permute-start(f32[2,7,72,128]{3,2,1,0:T(8,128)S(1)} %get-tuple-element.56), channel_id=1, source_target_pairs={{0,1},{1,9},{2,3},{3,11},{4,5},{5,13},{6,7},{7,15},{8,0},{9,8},{10... | collective-permute-start | bytes 1548296 | tf_op jit(solution)/shard_map/ppermute | solution.py:300
  10.7 7.7 %collective-permute-start.4 = (f32[2,4,72,128]{3,2,1,0:T(8,128)S(1)}, f32[2,4,72,128]{3,2,1,0:T(8,128)S(1)}, u32[]{:S(2)}, u32[]{:S(2)}) collective-permute-start(f32[2,4,72,128]{3,2,1,0:T(8,128)S(1)} %get-tuple-element.55), channel_id=1, source_target_pairs={{0,0},{1,8},{2,2},{3,10},{4,4},{5,12},{6,6},{7,14},{8,1},{9,9},{10... | collective-permute-start | bytes 884744 | tf_op jit(solution)/shard_map/ppermute | solution.py:300
  14.2 8.8 %collective-permute-start.6 = (f32[2,4,72,128]{3,2,1,0:T(8,128)S(1)}, f32[2,4,72,128]{3,2,1,0:T(8,128)S(1)}, u32[]{:S(2)}, u32[]{:S(2)}) collective-permute-start(f32[2,4,72,128]{3,2,1,0:T(8,128)S(1)} %get-tuple-element.53.field.other), channel_id=1, source_target_pairs={{0,8},{1,9},{2,10},{3,11},{4,12},{5,13},{6,14},{7,15},{8,0},{9,1},... | collective-permute-start | bytes 884744 | tf_op jit(solution)/shard_map/ppermute | solution.py:300
  15.3 11.2 %collective-permute-start.2 = (f32[2,4,72,128]{3,2,1,0:T(8,128)S(1)}, f32[2,4,72,128]{3,2,1,0:T(8,128)S(1)}, u32[]{:S(2)}, u32[]{:S(2)}) collective-permute-start(f32[2,4,72,128]{3,2,1,0:T(8,128)S(1)} %get-tuple-element.52.other.field), channel_id=1, source_target_pairs={{0,1},{1,0},{2,8},{3,9},{4,10},{5,11},{6,12},{7,13},{8,2},{9,3},{1... | collective-permute-start | bytes 884744 | tf_op jit(solution)/shard_map/ppermute | solution.py:300
  16.9 6.2 %collective-permute-start.3 = (f32[2,72,128]{2,1,0:T(8,128)S(1)}, f32[2,72,128]{2,1,0:T(8,128)S(1)}, u32[]{:S(2)}, u32[]{:S(2)}) collective-permute-start(f32[2,72,128]{2,1,0:T(8,128)S(1)} %get-tuple-element.54), channel_id=1, source_target_pairs={{0,16},{1,17},{2,18},{3,19},{4,20},{5,21},{6,22},{7,23},{8,24},{9,... | collective-permute-start | bytes 221192 | tf_op jit(solution)/shard_map/ppermute | solution.py:300
  23.9 9.3 %collective-permute-start.9 = (f32[2,4,72,128]{3,2,1,0:T(8,128)S(1)}, f32[2,4,72,128]{3,2,1,0:T(8,128)S(1)}, u32[]{:S(2)}, u32[]{:S(2)}) collective-permute-start(f32[2,4,72,128]{3,2,1,0:T(8,128)S(1)} %get-tuple-element.65.field.other), channel_id=1, source_target_pairs={{0,8},{1,9},{2,10},{3,11},{4,12},{5,13},{6,14},{7,15},{8,0},{9,1},... | collective-permute-start | bytes 884744 | tf_op jit(solution)/shard_map/ppermute | solution.py:300
  27.4 6.8 %collective-permute-start.7 = (f32[2,4,72,128]{3,2,1,0:T(8,128)S(1)}, f32[2,4,72,128]{3,2,1,0:T(8,128)S(1)}, u32[]{:S(2)}, u32[]{:S(2)}) collective-permute-start(f32[2,4,72,128]{3,2,1,0:T(8,128)S(1)} %get-tuple-element.64.other.field), channel_id=1, source_target_pairs={{0,1},{1,0},{2,8},{3,9},{4,10},{5,11},{6,12},{7,13},{8,2},{9,3},{1... | collective-permute-start | bytes 884744 | tf_op jit(solution)/shard_map/ppermute | solution.py:300
  34.1 6.8 %collective-permute-start.12 = (f32[2,4,72,128]{3,2,1,0:T(8,128)S(1)}, f32[2,4,72,128]{3,2,1,0:T(8,128)S(1)}, u32[]{:S(2)}, u32[]{:S(2)}) collective-permute-start(f32[2,4,72,128]{3,2,1,0:T(8,128)S(1)} %get-tuple-element.69.field.other.refs_0_), channel_id=1, source_target_pairs={{0,8},{1,9},{2,10},{3,11},{4,12},{5,13},{6,14},{7,15},{8,0},{9,1},... | collective-permute-start | bytes 884744 | tf_op jit(solution)/shard_map/ppermute | solution.py:300
  35.1 6.8 %collective-permute-start.10 = (f32[2,4,72,128]{3,2,1,0:T(8,128)S(1)}, f32[2,4,72,128]{3,2,1,0:T(8,128)S(1)}, u32[]{:S(2)}, u32[]{:S(2)}) collective-permute-start(f32[2,4,72,128]{3,2,1,0:T(8,128)S(1)} %get-tuple-element.68.other.field.refs_0_), channel_id=1, source_target_pairs={{0,1},{1,0},{2,8},{3,9},{4,10},{5,11},{6,12},{7,13},{8,2},{9,3},{1... | collective-permute-start | bytes 884744 | tf_op jit(solution)/shard_map/ppermute | solution.py:300
  36.6 4.4 %collective-permute-start.11 = (f32[2,72,128]{2,1,0:T(8,128)S(1)}, f32[2,72,128]{2,1,0:T(8,128)S(1)}, u32[]{:S(2)}, u32[]{:S(2)}) collective-permute-start(f32[2,72,128]{2,1,0:T(8,128)S(1)} %get-tuple-element.70), channel_id=1, source_target_pairs={{0,16},{1,17},{2,18},{3,19},{4,20},{5,21},{6,22},{7,23},{8,24},{9,... | collective-permute-start | bytes 221192 | tf_op jit(solution)/shard_map/ppermute | solution.py:300
  41.8 6.8 %collective-permute-start.15 = (f32[4,72,128]{2,1,0:T(8,128)S(1)}, f32[4,72,128]{2,1,0:T(8,128)S(1)}, u32[]{:S(2)}, u32[]{:S(2)}) collective-permute-start(f32[4,72,128]{2,1,0:T(8,128)S(1)} %get-tuple-element.75.field.other), channel_id=1, source_target_pairs={{0,8},{1,9},{2,10},{3,11},{4,12},{5,13},{6,14},{7,15},{8,0},{9,1},... | collective-permute-start | bytes 442376 | tf_op jit(solution)/shard_map/ppermute | solution.py:300
  42.7 6.6 %collective-permute-start.13 = (f32[4,72,128]{2,1,0:T(8,128)S(1)}, f32[4,72,128]{2,1,0:T(8,128)S(1)}, u32[]{:S(2)}, u32[]{:S(2)}) collective-permute-start(f32[4,72,128]{2,1,0:T(8,128)S(1)} %get-tuple-element.74.other.field), channel_id=1, source_target_pairs={{0,1},{1,0},{2,8},{3,9},{4,10},{5,11},{6,12},{7,13},{8,2},{9,3},{1... | collective-permute-start | bytes 442376 | tf_op jit(solution)/shard_map/ppermute | solution.py:300
  49.3 5.9 %collective-permute-start.18 = (f32[4,72,128]{2,1,0:T(8,128)S(1)}, f32[4,72,128]{2,1,0:T(8,128)S(1)}, u32[]{:S(2)}, u32[]{:S(2)}) collective-permute-start(f32[4,72,128]{2,1,0:T(8,128)S(1)} %get-tuple-element.81.field.other), channel_id=1, source_target_pairs={{0,8},{1,9},{2,10},{3,11},{4,12},{5,13},{6,14},{7,15},{8,0},{9,1},... | collective-permute-start | bytes 442376 | tf_op jit(solution)/shard_map/ppermute | solution.py:300
  50.1 5.9 %collective-permute-start.16 = (f32[4,72,128]{2,1,0:T(8,128)S(1)}, f32[4,72,128]{2,1,0:T(8,128)S(1)}, u32[]{:S(2)}, u32[]{:S(2)}) collective-permute-start(f32[4,72,128]{2,1,0:T(8,128)S(1)} %get-tuple-element.80.other.field), channel_id=1, source_target_pairs={{0,1},{1,0},{2,8},{3,9},{4,10},{5,11},{6,12},{7,13},{8,2},{9,3},{1... | collective-permute-start | bytes 442376 | tf_op jit(solution)/shard_map/ppermute | solution.py:300
  56.0 6.7 %collective-permute-start.21 = (f32[2,4,72,128]{3,2,1,0:T(8,128)S(1)}, f32[2,4,72,128]{3,2,1,0:T(8,128)S(1)}, u32[]{:S(2)}, u32[]{:S(2)}) collective-permute-start(f32[2,4,72,128]{3,2,1,0:T(8,128)S(1)} %get-tuple-element.85.field.other), channel_id=1, source_target_pairs={{0,8},{1,9},{2,10},{3,11},{4,12},{5,13},{6,14},{7,15},{8,0},{9,1},... | collective-permute-start | bytes 884744 | tf_op jit(solution)/shard_map/ppermute | solution.py:300
  56.9 6.8 %collective-permute-start.19 = (f32[2,4,72,128]{3,2,1,0:T(8,128)S(1)}, f32[2,4,72,128]{3,2,1,0:T(8,128)S(1)}, u32[]{:S(2)}, u32[]{:S(2)}) collective-permute-start(f32[2,4,72,128]{3,2,1,0:T(8,128)S(1)} %get-tuple-element.84.other.field), channel_id=1, source_target_pairs={{0,1},{1,0},{2,8},{3,9},{4,10},{5,11},{6,12},{7,13},{8,2},{9,3},{1... | collective-permute-start | bytes 884744 | tf_op jit(solution)/shard_map/ppermute | solution.py:300
  58.3 4.4 %collective-permute-start.20 = (f32[2,72,128]{2,1,0:T(8,128)S(1)}, f32[2,72,128]{2,1,0:T(8,128)S(1)}, u32[]{:S(2)}, u32[]{:S(2)}) collective-permute-start(f32[2,72,128]{2,1,0:T(8,128)S(1)} %get-tuple-element.86), channel_id=1, source_target_pairs={{0,16},{1,17},{2,18},{3,19},{4,20},{5,21},{6,22},{7,23},{8,24},{9,... | collective-permute-start | bytes 221192 | tf_op jit(solution)/shard_map/ppermute | solution.py:300
  63.6 6.8 %collective-permute-start.26 = (f32[2,4,72,128]{3,2,1,0:T(8,128)S(1)}, f32[2,4,72,128]{3,2,1,0:T(8,128)S(1)}, u32[]{:S(2)}, u32[]{:S(2)}) collective-permute-start(f32[2,4,72,128]{3,2,1,0:T(8,128)S(1)} %get-tuple-element.89.other.field), channel_id=1, source_target_pairs={{0,8},{1,9},{2,10},{3,11},{4,12},{5,13},{6,14},{7,15},{8,0},{9,1},... | collective-permute-start | bytes 884744 | tf_op jit(solution)/shard_map/ppermute | solution.py:300
  64.5 10.0 %collective-permute-start.22 = (f32[2,4,72,128]{3,2,1,0:T(8,128)S(1)}, f32[2,4,72,128]{3,2,1,0:T(8,128)S(1)}, u32[]{:S(2)}, u32[]{:S(2)}) collective-permute-start(f32[2,4,72,128]{3,2,1,0:T(8,128)S(1)} %get-tuple-element.88.field.other), channel_id=1, source_target_pairs={{0,1},{1,0},{2,8},{3,9},{4,10},{5,11},{6,12},{7,13},{8,2},{9,3},{1... | collective-permute-start | bytes 884744 | tf_op jit(solution)/shard_map/ppermute | solution.py:300
  71.8 6.3 %collective-permute-start.27 = (f32[4,64,128]{2,1,0:T(8,128)S(1)}, f32[4,64,128]{2,1,0:T(8,128)S(1)}, u32[]{:S(2)}, u32[]{:S(2)}) collective-permute-start(f32[4,64,128]{2,1,0:T(8,128)S(1)} %get-tuple-element.93), channel_id=1, source_target_pairs={{0,0},{1,8},{2,2},{3,10},{4,4},{5,12},{6,6},{7,14},{8,1},{9,9},{10... | collective-permute-start | bytes 393224 | tf_op jit(solution)/shard_map/ppermute | solution.py:300
  72.5 6.2 %collective-permute-start.28 = (f32[4,64,128]{2,1,0:T(8,128)S(1)}, f32[4,64,128]{2,1,0:T(8,128)S(1)}, u32[]{:S(2)}, u32[]{:S(2)}) collective-permute-start(f32[4,64,128]{2,1,0:T(8,128)S(1)} %get-tuple-element.94), channel_id=1, source_target_pairs={{0,8},{1,0},{2,10},{3,2},{4,12},{5,4},{6,14},{7,6},{8,9},{9,1},{10... | collective-permute-start | bytes 393224 | tf_op jit(solution)/shard_map/ppermute | solution.py:300
  76.7 7.2 %collective-permute-start.25 = (f32[4,64,128]{2,1,0:T(8,128)S(1)}, f32[4,64,128]{2,1,0:T(8,128)S(1)}, u32[]{:S(2)}, u32[]{:S(2)}) collective-permute-start(f32[4,64,128]{2,1,0:T(8,128)S(1)} %get-tuple-element.92), channel_id=1, source_target_pairs={{0,8},{1,0},{2,10},{3,2},{4,12},{5,4},{6,14},{7,6},{8,9},{9,1},{10... | collective-permute-start | bytes 393224 | tf_op jit(solution)/shard_map/ppermute | solution.py:300
  (12 other events, 40.5 us)
